TPU v7x, 32 devices: a whole 2x2x4 slice. The times are simulated.
32 devices in a mesh: blk: 16 (over z, y, x), row: 2 (over core).
Axes of the slice: x: 2, y: 2, z: 4, core: 2. Of those that a mesh axis runs over, the one named last changes fastest.
Arguments:
- genotypes: bfloat16 [128, 16, 2048], P('blk', None, 'row'), may hold values from 0 to 2
- assignment: int32 [16], replicated, may hold values from 0 to 15, each once
- snp_counts: int32 [16], replicated, may hold values from 1024 to 2048, as said below
- basis: float32 [16, 64, 2048], P('blk', None, 'row'), may hold values from -6 to 6
Outputs:
- image: float32 [16, 64, 2048], P('blk', None, 'row')
- new_basis: float32 [16, 64, 2048], P('blk', None, 'row')
- factor: float32 [16, 64, 64], P('blk')
Inputs may be any that keep to these rules, and one draw needn't show every extreme that they name: `assignment`: each block number appears exactly once. `snp_counts`: A block's SNPs fill its leading slots.
All inputs are finite; a program needn't handle non-finite values.
Results may differ from a plain program's by a relative error of at most 0.0021.
Values may be sent and summed in bfloat16 or wider, within the bound.
No kernel may reach another device: no remote copies, remote signals or barrier semaphores. Data moves between devices by JAX's collectives and lax.ppermute only.
A program may use at most 64 MiB of HBM per device.

v0:
```python
import jax
import jax.numpy as jnp
from jax import lax
from jax.sharding import PartitionSpec as P

epsilon = 1e-05
shrink_weight = 0.5


def body(genotypes, assignment, snp_counts, basis):
    ordered = jnp.take(genotypes, assignment, axis=1)
    regrouped = lax.all_to_all(ordered, "blk", split_axis=1, concat_axis=0, tiled=True)
    samples = regrouped.shape[0]
    owned = regrouped.shape[1]
    half_width = regrouped.shape[2]
    block_ids = lax.dynamic_slice_in_dim(assignment, lax.axis_index("blk") * owned, owned)
    catalog = jnp.arange(snp_counts.shape[0], dtype=jnp.int32)
    live_count = jnp.sum(
        jnp.where(block_ids[:, None] == catalog[None, :], snp_counts[None, :], 0), axis=1
    )
    columns = lax.axis_index("row") * half_width + jnp.arange(half_width, dtype=jnp.int32)
    live_mask = columns[None, :] < live_count[:, None]
    values = regrouped.astype(jnp.float32)
    col_mean = jnp.mean(values, axis=0)
    centered = values - col_mean[None]
    col_var = jnp.mean(centered * centered, axis=0)
    standard = jnp.where(
        live_mask[None], centered * lax.rsqrt(col_var + epsilon)[None], 0.0
    ).astype(jnp.bfloat16)
    inverse = 1.0 / samples
    partial_proj = jnp.einsum(
        "nbi,bri->brn",
        standard,
        basis,
        precision=lax.Precision.HIGHEST,
        preferred_element_type=jnp.float32,
    )
    projected = lax.psum(partial_proj, "row")
    product = (
        jnp.einsum(
            "nbi,brn->bri",
            standard,
            projected,
            precision=lax.Precision.HIGHEST,
            preferred_element_type=jnp.float32,
        )
        * inverse
    )
    image = shrink_weight * product + (1.0 - shrink_weight) * jnp.where(
        live_mask[:, None, :], basis, 0.0
    )
    gram_part = jnp.einsum("bri,bsi->brs", image, image, precision=lax.Precision.HIGHEST)
    gram_sum = lax.psum(gram_part, "row")
    factor = jnp.linalg.cholesky(gram_sum)
    new_basis = jax.scipy.linalg.solve_triangular(factor, image, lower=True)
    return (image, new_basis, factor)


def solution(mesh):
    in_specs = (P("blk", None, "row"), P(), P(), P("blk", None, "row"))
    out_specs = (P("blk", None, "row"), P("blk", None, "row"), P("blk", None, None))
    return jax.shard_map(body, mesh=mesh, in_specs=in_specs, out_specs=out_specs, check_vma=False)
```

profile of v0, /device:TPU:0, one launch (start us, length us, event | category | flops | bytes accessed | tf_op | source)
XLA Modules:
  0.0 44.3 jit_solution(11214147400684434349)
XLA Ops:
  0.7 0.7 %compare_and_fusion = pred[16]{0:T(512)(128)(4,1)S(1)} fusion(s32[16]{0:T(128)} %param.5), kind=kLoop, calls=%fused_computation.36 | loop fusion | flops 96 | bytes 80 | tf_op jit(solution)/shard_map/jit(_take)/and | solution.py:11
  1.4 0.2 copy-done
  1.6 1.3 %gather_fusion = bf16[16,8,1024]{2,0,1:T(8,128)(2,1)S(1)} fusion(bf16[8,16,1024]{2,1,0:T(8,128)(2,1)S(1)} %copy-done, s32[1024]{0:T(1024)S(1)} %pad_clamp_fusion), kind=kCustom, calls=%fused_computation | custom fusion | bytes 524352 | tf_op jit(solution)/shard_map/jit(_take)/gather | solution.py:11
  2.9 0.1 select_bitcast_fusion
  3.0 0.9 %copy.13 = bf16[8,16,1024]{2,0,1:T(8,128)(2,1)} copy(bf16[8,16,1024]{2,1,0:T(8,128)(2,1)S(1)} %select_bitcast_fusion) | data formatting | bytes 524288 | tf_op jit(solution)/shard_map/jit(_take)/select_n | solution.py:11
  3.9 8.3 %all-to-all-start = ((bf16[8,16,1024]{2,0,1:T(8,128)(2,1)}), bf16[8,16,1024]{2,0,1:T(8,128)(2,1)S(1)}, u32[]{:S(2)}, u32[]{:S(2)}) async-start(bf16[8,16,1024]{2,0,1:T(8,128)(2,1)} %copy.13), calls=%async_computation | async-start | bytes 524288 | tf_op jit(solution)/shard_map/all_to_all | solution.py:12
  12.2 0.6 %dynamic_slice.3 = s32[1]{0:T(128)} dynamic-slice(s32[16]{0:T(128)S(1)} %copy-done.3, s32[]{:T(128)S(6)} %select_n.50), dynamic_slice_sizes={1} | dynamic-slice | bytes 12 | tf_op jit(solution)/shard_map/dynamic_slice | solution.py:16
  12.8 0.7 %copy-done.4 = s32[16]{0:T(128)S(1)} copy-done((s32[16]{0:T(128)S(1)}, s32[16]{0:T(128)}, u32[]{:S(2)}) %copy-start.4) | copy-done | bytes 88
  13.5 1.3 %fusion.18 = s32[]{:T(128)} fusion(s32[16]{0:T(128)S(1)} %copy-done.4, s32[]{:T(128)} %bitcast), kind=kLoop, calls=%fused_computation.38 | loop fusion | flops 47 | bytes 72 | tf_op jit(solution)/shard_map/reduce_sum | solution.py:18
  14.8 0.7 %add_compare_fusion = pred[1024]{0:T(1024)(128)(4,1)S(1)} fusion(s32[]{:T(128)} %fusion.18, s32[]{:T(128)S(6)} %mul.56), kind=kLoop, calls=%fused_computation.32 | loop fusion | flops 2048 | bytes 1032 | tf_op jit(solution)/shard_map/lt | solution.py:22
  15.4 6.7 %all-to-all-done = bf16[8,16,1024]{2,0,1:T(8,128)(2,1)S(1)} async-done(((bf16[8,16,1024]{2,0,1:T(8,128)(2,1)}), bf16[8,16,1024]{2,0,1:T(8,128)(2,1)S(1)}, u32[]{:S(2)}, u32[]{:S(2)}) %all-to-all-start) | async-done | bytes 262176 | tf_op jit(solution)/shard_map/all_to_all | solution.py:12
  22.1 0.1 convert_reduce_fusion
  22.2 0.1 fusion.4
  22.3 0.4 convolution_bitcast_fusion.2
  22.7 3.4 %psum.14 = f32[64,128]{1,0:T(8,128)S(1)} all-reduce(f32[64,128]{1,0:T(8,128)S(1)} %convolution_bitcast_fusion.2), channel_id=1, replica_groups=mesh['blk'=16,'row'=2] {'row'}, use_global_device_ids=true, to_apply=%region_3.4 | all-reduce | flops 8192 | bytes 65536 | tf_op jit(solution)/shard_map/psum | solution.py:38
  26.1 0.3 fusion.1
  26.4 0.4 convolution_bitcast_fusion.1
  26.8 3.6 %psum.15 = f32[1,64,64]{1,2,0:T(8,128)S(1)} all-reduce(f32[1,64,64]{1,2,0:T(8,128)S(1)} %convolution_bitcast_fusion.1), channel_id=1, replica_groups=mesh['blk'=16,'row'=2] {'row'}, use_global_device_ids=true, to_apply=%region_4.5 | all-reduce | flops 4096 | bytes 32768 | tf_op jit(solution)/shard_map/psum | solution.py:53
  30.3 0.1 copy.15
  30.4 5.8 %custom-call.8 = f32[1,64,64]{2,1,0:T(8,128)S(1)} custom-call(f32[1,64,64]{2,1,0:T(8,128)S(1)} %fusion.16), custom_call_target="Cholesky" | custom-call | tf_op jit(solution)/shard_map/jit(cholesky)/cholesky | solution.py:54
  36.3 0.6 %compare_reduce_fusion = pred[]{:T(512)} fusion(f32[64]{0:T(128)S(1)} %select_reduce_fusion), kind=kLoop, calls=%fused_computation.35 | loop fusion | flops 127 | bytes 257 | tf_op jit(solution)/shard_map/jit(cholesky)/cholesky | solution.py:54
  37.0 1.3 %fusion.17 = (f32[1,64,64]{2,1,0:T(8,128)S(1)}, f32[1,64,64]{2,1,0:T(8,128)}) fusion(f32[1,64,64]{2,1,0:T(8,128)S(1)} %custom-call.8, pred[]{:T(512)} %compare_reduce_fusion), kind=kLoop, calls=%fused_computation.29 | loop fusion | flops 16384 | bytes 49153 | tf_op jit(solution)/shard_map/jit(_solve_triangular)/triangular_solve | solution.py:55
  38.2 4.9 %custom-call.9 = f32[1,64,64]{1,2,0:T(8,128)S(1)} custom-call(f32[1,64,64]{2,1,0:T(8,128)S(1)} %get-tuple-element.3), custom_call_target="InvertDiagBlocksLowerTriangular" | custom-call | tf_op jit(solution)/shard_map/jit(_solve_triangular)/triangular_solve | solution.py:55
  43.1 1.1 %convolution_bitcast_fusion = f32[1,64,1024]{2,1,0:T(8,128)} fusion(f32[1,64,1024]{2,1,0:T(8,128)S(1)} %fusion.1, f32[1,64,64]{1,2,0:T(8,128)S(1)} %custom-call.9), kind=kOutput, calls=%fused_computation.3 | convolution fusion | flops 50331648 | bytes 540672 | tf_op jit(solution)/shard_map/jit(_solve_triangular)/triangular_solve | solution.py:55
  (14 shorter events, 0.1 us)
Async XLA Ops:
  0.6 1.0 %copy-start = (bf16[8,16,1024]{2,1,0:T(8,128)(2,1)S(1)}, bf16[8,16,1024]{2,1,0:T(8,128)(2,1)}, u32[]{:S(2)}) copy-start(bf16[8,16,1024]{2,1,0:T(8,128)(2,1)} %param.4) | copy-start | bytes 786436
  0.6 0.7 %copy-start.3 = (s32[16]{0:T(128)S(1)}, s32[16]{0:T(128)}, u32[]{:S(2)}) copy-start(s32[16]{0:T(128)} %param.5) | copy-start | bytes 196
  3.9 18.2 %all-to-all-start = ((bf16[8,16,1024]{2,0,1:T(8,128)(2,1)}), bf16[8,16,1024]{2,0,1:T(8,128)(2,1)S(1)}, u32[]{:S(2)}, u32[]{:S(2)}) async-start(bf16[8,16,1024]{2,0,1:T(8,128)(2,1)} %copy.13), calls=%async_computation | async-start | bytes 524288 | tf_op jit(solution)/shard_map/all_to_all | solution.py:12
  12.8 0.7 %copy-start.4 = (s32[16]{0:T(128)S(1)}, s32[16]{0:T(128)}, u32[]{:S(2)}) copy-start(s32[16]{0:T(128)} %param.6) | copy-start | bytes 196
  15.4 6.9 %copy-start.2 = (f32[1,64,1024]{2,1,0:T(8,128)S(1)}, f32[1,64,1024]{2,1,0:T(8,128)}, u32[]{:S(2)}) copy-start(f32[1,64,1024]{2,1,0:T(8,128)} %param.7) | copy-start | bytes 786436
  26.4 16.8 %copy-start.1 = (f32[1,64,1024]{2,1,0:T(8,128)}, f32[1,64,1024]{2,1,0:T(8,128)S(1)}, u32[]{:S(2)}) copy-start(f32[1,64,1024]{2,1,0:T(8,128)S(1)} %fusion.1) | copy-start | bytes 786436
where the time goes:
time: 44.6 us; the launch traced here: 44.3 us
  other arithmetic  15.6 us (35%)
  starting transfers between devices  8.34 us (19%)
  blocking collectives  6.97 us (16%)
  waiting for transfers between devices  6.68 us (15%)
  local copies, waits for them, and re-layouts  3.73 us (8%)
  matrix products  2.15 us (5%)
  between operations  0.79 us (2%)
    all_to_all x1, starting transfers between devices, body(): lax.all_to_all(ordered, 'blk', split_axis=1, concat_axis=0, tiled=True)  8.34 us
    all_to_all x1, waiting for transfers between devices, body(): lax.all_to_all(ordered, 'blk', split_axis=1, concat_axis=0, tiled=True)  6.68 us
    another operation x3, other arithmetic, body(): factor = jnp.linalg.cholesky(gram_sum)  6.52 us
    another operation x2, other arithmetic, body(): new_basis = jax.scipy.linalg.solve_triangular(factor, image, lower=True)  6.16 us
    psum x1, blocking collectives, body(): gram_sum = lax.psum(gram_part, 'row')  3.57 us
    psum x1, blocking collectives, body(): projected = lax.psum(partial_proj, 'row')  3.41 us
    gather x1, local copies, waits for them, and re-layouts, body(): ordered = jnp.take(genotypes, assignment, axis=1)  1.31 us
    reduce_sum x1, other arithmetic, body(): jnp.sum(jnp.where(block_ids[:, None] == catalog[None, :], snp_counts[None...  1.27 us
  transfers between devices with their start and end apart: 1, of which 1 were waited for; matrix products, arithmetic and copies ran while one was open for 6% of the time, Pallas kernels for 0%

commit v1 on v0

--- a/solution.py
+++ b/solution.py
@@ -50,7 +50,7 @@
         live_mask[:, None, :], basis, 0.0
     )
     gram_part = jnp.einsum("bri,bsi->brs", image, image, precision=lax.Precision.HIGHEST)
-    gram_sum = lax.psum(gram_part, "row")
+    gram_sum = jnp.sum(lax.all_gather(gram_part, "row"), axis=0)
     factor = jnp.linalg.cholesky(gram_sum)
     new_basis = jax.scipy.linalg.solve_triangular(factor, image, lower=True)
     return (image, new_basis, factor)

time: 44.6 us -> 43 us (0.964)
  blocking collectives: 6.97 us -> 5.26 us
    psum x1 -> x0, blocking collectives: 3.57 us -> none  [body(): gram_sum = lax.psum(gram_part, 'row')]
    all_gather x0 -> x1, blocking collectives: none -> 1.85 us  [body(): gram_sum = jnp.sum(lax.all_gather(gram_part, 'row'), axis=0)]
where the time goes in v1:
time: 43 us; the launch traced here: 42.6 us
  other arithmetic  15.6 us (36%)
  starting transfers between devices  8.34 us (19%)
  waiting for transfers between devices  6.68 us (16%)
  blocking collectives  5.26 us (12%)
  local copies, waits for them, and re-layouts  3.8 us (9%)
  matrix products  2.14 us (5%)
  between operations  0.78 us (2%)
    all_to_all x1, starting transfers between devices, body(): lax.all_to_all(ordered, 'blk', split_axis=1, concat_axis=0, tiled=True)  8.34 us
    all_to_all x1, waiting for transfers between devices, body(): lax.all_to_all(ordered, 'blk', split_axis=1, concat_axis=0, tiled=True)  6.68 us
    another operation x3, other arithmetic, body(): factor = jnp.linalg.cholesky(gram_sum)  6.52 us
    another operation x2, other arithmetic, body(): new_basis = jax.scipy.linalg.solve_triangular(factor, image, lower=True)  6.16 us
    psum x1, blocking collectives, body(): projected = lax.psum(partial_proj, 'row')  3.41 us
    all_gather x1, blocking collectives, body(): gram_sum = jnp.sum(lax.all_gather(gram_part, 'row'), axis=0)  1.85 us
    gather x1, local copies, waits for them, and re-layouts, body(): ordered = jnp.take(genotypes, assignment, axis=1)  1.31 us
    reduce_sum x1, other arithmetic, body(): jnp.sum(jnp.where(block_ids[:, None] == catalog[None, :], snp_counts[None...  1.27 us
  transfers between devices with their start and end apart: 1, of which 1 were waited for; matrix products, arithmetic and copies ran while one was open for 6% of the time, Pallas kernels for 0%

profile of v1, /device:TPU:0, one launch (start us, length us, event | category | flops | bytes accessed | tf_op | source)
XLA Modules:
  0.0 42.6 jit_solution(2016626861580508904)
XLA Ops:
  0.7 0.7 %compare_and_fusion = pred[16]{0:T(512)(128)(4,1)S(1)} fusion(s32[16]{0:T(128)} %param.5), kind=kLoop, calls=%fused_computation.36 | loop fusion | flops 96 | bytes 80 | tf_op jit(solution)/shard_map/jit(_take)/and | solution.py:11
  1.4 0.2 copy-done
  1.6 1.3 %gather_fusion = bf16[16,8,1024]{2,0,1:T(8,128)(2,1)S(1)} fusion(bf16[8,16,1024]{2,1,0:T(8,128)(2,1)S(1)} %copy-done, s32[1024]{0:T(1024)S(1)} %pad_clamp_fusion), kind=kCustom, calls=%fused_computation | custom fusion | bytes 524352 | tf_op jit(solution)/shard_map/jit(_take)/gather | solution.py:11
  2.9 0.1 select_bitcast_fusion
  3.0 0.9 %copy.11 = bf16[8,16,1024]{2,0,1:T(8,128)(2,1)} copy(bf16[8,16,1024]{2,1,0:T(8,128)(2,1)S(1)} %select_bitcast_fusion) | data formatting | bytes 524288 | tf_op jit(solution)/shard_map/jit(_take)/select_n | solution.py:11
  3.9 8.3 %all-to-all-start = ((bf16[8,16,1024]{2,0,1:T(8,128)(2,1)}), bf16[8,16,1024]{2,0,1:T(8,128)(2,1)S(1)}, u32[]{:S(2)}, u32[]{:S(2)}) async-start(bf16[8,16,1024]{2,0,1:T(8,128)(2,1)} %copy.11), calls=%async_computation | async-start | bytes 524288 | tf_op jit(solution)/shard_map/all_to_all | solution.py:12
  12.2 0.6 %dynamic_slice.3 = s32[1]{0:T(128)} dynamic-slice(s32[16]{0:T(128)S(1)} %copy-done.3, s32[]{:T(128)S(6)} %select_n.50), dynamic_slice_sizes={1} | dynamic-slice | bytes 12 | tf_op jit(solution)/shard_map/dynamic_slice | solution.py:16
  12.8 0.7 %copy-done.4 = s32[16]{0:T(128)S(1)} copy-done((s32[16]{0:T(128)S(1)}, s32[16]{0:T(128)}, u32[]{:S(2)}) %copy-start.4) | copy-done | bytes 88
  13.5 1.3 %fusion.19 = s32[]{:T(128)} fusion(s32[16]{0:T(128)S(1)} %copy-done.4, s32[]{:T(128)} %bitcast), kind=kLoop, calls=%fused_computation.38 | loop fusion | flops 47 | bytes 72 | tf_op jit(solution)/shard_map/reduce_sum | solution.py:18
  14.8 0.7 %add_compare_fusion = pred[1024]{0:T(1024)(128)(4,1)S(1)} fusion(s32[]{:T(128)} %fusion.19, s32[]{:T(128)S(6)} %mul.56), kind=kLoop, calls=%fused_computation.32 | loop fusion | flops 2048 | bytes 1032 | tf_op jit(solution)/shard_map/lt | solution.py:22
  15.4 6.7 %all-to-all-done = bf16[8,16,1024]{2,0,1:T(8,128)(2,1)S(1)} async-done(((bf16[8,16,1024]{2,0,1:T(8,128)(2,1)}), bf16[8,16,1024]{2,0,1:T(8,128)(2,1)S(1)}, u32[]{:S(2)}, u32[]{:S(2)}) %all-to-all-start) | async-done | bytes 262176 | tf_op jit(solution)/shard_map/all_to_all | solution.py:12
  22.2 0.1 fusion.4
  22.3 0.4 convolution_bitcast_fusion.1
  22.7 3.4 %psum.7 = f32[64,128]{1,0:T(8,128)S(1)} all-reduce(f32[64,128]{1,0:T(8,128)S(1)} %convolution_bitcast_fusion.1), channel_id=1, replica_groups=mesh['blk'=16,'row'=2] {'row'}, use_global_device_ids=true, to_apply=%region_3.4 | all-reduce | flops 8192 | bytes 65536 | tf_op jit(solution)/shard_map/psum | solution.py:38
  26.1 0.3 fusion.1
  26.4 0.4 fusion.11
  26.8 1.9 %all-gather = f32[128,64]{1,0:T(8,128)S(1)} all-gather(f32[64,64]{1,0:T(8,128)S(1)} %fusion.11), channel_id=2, replica_groups=mesh['blk'=16,'row'=2] {'row'}, dimensions={0}, use_global_device_ids=true | all-gather | bytes 49152 | tf_op jit(solution)/shard_map/all_gather | solution.py:53
  28.6 0.1 copy.12
  28.7 0.1 copy.13
  28.8 5.8 %custom-call.8 = f32[1,64,64]{2,1,0:T(8,128)S(1)} custom-call(f32[1,64,64]{2,1,0:T(8,128)S(1)} %fusion.16), custom_call_target="Cholesky" | custom-call | tf_op jit(solution)/shard_map/jit(cholesky)/cholesky | solution.py:54
  34.7 0.6 %compare_reduce_fusion = pred[]{:T(512)} fusion(f32[64]{0:T(128)S(1)} %select_reduce_fusion), kind=kLoop, calls=%fused_computation.35 | loop fusion | flops 127 | bytes 257 | tf_op jit(solution)/shard_map/jit(cholesky)/cholesky | solution.py:54
  35.3 1.3 %fusion.18 = (f32[1,64,64]{2,1,0:T(8,128)S(1)}, f32[1,64,64]{2,1,0:T(8,128)}) fusion(f32[1,64,64]{2,1,0:T(8,128)S(1)} %custom-call.8, pred[]{:T(512)} %compare_reduce_fusion), kind=kLoop, calls=%fused_computation.29 | loop fusion | flops 16384 | bytes 49153 | tf_op jit(solution)/shard_map/jit(_solve_triangular)/triangular_solve | solution.py:55
  36.6 4.9 %custom-call.9 = f32[1,64,64]{1,2,0:T(8,128)S(1)} custom-call(f32[1,64,64]{2,1,0:T(8,128)S(1)} %get-tuple-element.3), custom_call_target="InvertDiagBlocksLowerTriangular" | custom-call | tf_op jit(solution)/shard_map/jit(_solve_triangular)/triangular_solve | solution.py:55
  41.5 1.1 %convolution_bitcast_fusion = f32[1,64,1024]{2,1,0:T(8,128)} fusion(f32[1,64,1024]{2,1,0:T(8,128)S(1)} %fusion.1, f32[1,64,64]{1,2,0:T(8,128)S(1)} %custom-call.9), kind=kOutput, calls=%fused_computation.3 | convolution fusion | flops 50331648 | bytes 540672 | tf_op jit(solution)/shard_map/jit(_solve_triangular)/triangular_solve | solution.py:55
  (16 shorter events, 0.2 us)
Async XLA Ops:
  0.6 1.0 %copy-start = (bf16[8,16,1024]{2,1,0:T(8,128)(2,1)S(1)}, bf16[8,16,1024]{2,1,0:T(8,128)(2,1)}, u32[]{:S(2)}) copy-start(bf16[8,16,1024]{2,1,0:T(8,128)(2,1)} %param.4) | copy-start | bytes 786436
  0.6 0.7 %copy-start.3 = (s32[16]{0:T(128)S(1)}, s32[16]{0:T(128)}, u32[]{:S(2)}) copy-start(s32[16]{0:T(128)} %param.5) | copy-start | bytes 196
  3.9 18.2 %all-to-all-start = ((bf16[8,16,1024]{2,0,1:T(8,128)(2,1)}), bf16[8,16,1024]{2,0,1:T(8,128)(2,1)S(1)}, u32[]{:S(2)}, u32[]{:S(2)}) async-start(bf16[8,16,1024]{2,0,1:T(8,128)(2,1)} %copy.11), calls=%async_computation | async-start | bytes 524288 | tf_op jit(solution)/shard_map/all_to_all | solution.py:12
  12.8 0.7 %copy-start.4 = (s32[16]{0:T(128)S(1)}, s32[16]{0:T(128)}, u32[]{:S(2)}) copy-start(s32[16]{0:T(128)} %param.6) | copy-start | bytes 196
  15.4 6.9 %copy-start.2 = (f32[1,64,1024]{2,1,0:T(8,128)S(1)}, f32[1,64,1024]{2,1,0:T(8,128)}, u32[]{:S(2)}) copy-start(f32[1,64,1024]{2,1,0:T(8,128)} %param.7) | copy-start | bytes 786436
  26.4 15.1 %copy-start.1 = (f32[1,64,1024]{2,1,0:T(8,128)}, f32[1,64,1024]{2,1,0:T(8,128)S(1)}, u32[]{:S(2)}) copy-start(f32[1,64,1024]{2,1,0:T(8,128)S(1)} %fusion.1) | copy-start | bytes 786436
